TPU v7x, 32 devices: a whole 2x2x4 slice. The times are simulated.
32 devices in a mesh: row: 8 (over z, x), col: 4 (over y, core).
Axes of the slice: x: 2, y: 2, z: 4, core: 2. Of those that a mesh axis runs over, the one named last changes fastest.
Arguments:
- grad: bfloat16 [16384, 1024], P(('row', 'col')), may hold values from -2500 to 2500
- left_root: bfloat16 [16384, 1024], P(('row', 'col')), may hold values from -0.051 to 3, as said below
- right_root: bfloat16 [16384, 1024], P(('row', 'col')), may hold values from -0.051 to 3, as said below
Outputs:
- update: bfloat16 [16384, 1024], P(('row', 'col'))
Inputs may be any that keep to these rules, and one draw needn't show every extreme that they name: `left_root`: each block L_b is symmetric and positive definite. `right_root`: each block R_b is symmetric and positive definite.
All inputs are finite; a program needn't handle non-finite values.
Results may differ from a plain program's by a relative error of at most 0.0049.
Values may be sent and summed in bfloat16 or wider, within the bound.
A program may use at most 64 MiB of HBM per device.

v0:
```python
import jax
import jax.numpy as jnp
from jax import lax
from jax.sharding import PartitionSpec as P

BLK = 1024


epsilon = 1e-06
clip_rms = 1.0


def partner(shard, axis, distance):
    return lax.ppermute(shard, axis, [(i, i ^ 1 << distance) for i in range(lax.axis_size(axis))])


def apply_right(gradient_rows, own_start, other_start, rows_here, right_root, partner_right):
    own_cols = lax.dynamic_slice_in_dim(gradient_rows, own_start, rows_here, 1)
    other_cols = lax.dynamic_slice_in_dim(gradient_rows, other_start, rows_here, 1)
    applied = jnp.dot(own_cols, right_root, preferred_element_type=jnp.float32)
    applied = applied + jnp.dot(other_cols, partner_right, preferred_element_type=jnp.float32)
    return applied.astype(jnp.bfloat16)


def shards(grad, left_root, right_root):
    rows_here = grad.shape[0]
    parity = lax.axis_index("col") % 2
    own_start = parity * rows_here
    other_start = (1 - parity) * rows_here
    partner_right = partner(right_root, "col", 0)
    right_applied = apply_right(grad, own_start, other_start, rows_here, right_root, partner_right)
    partner_rows = partner(right_applied, "col", 0)
    own_left = lax.dynamic_slice_in_dim(left_root, own_start, rows_here, 1)
    other_left = lax.dynamic_slice_in_dim(left_root, other_start, rows_here, 1)
    preconditioned = jnp.dot(own_left, right_applied, preferred_element_type=jnp.float32)
    preconditioned = preconditioned + jnp.dot(
        other_left, partner_rows, preferred_element_type=jnp.float32
    )
    grad_sq = jnp.sum(jnp.square(grad.astype(jnp.float32)))
    cond_sq = jnp.sum(preconditioned * preconditioned)
    global_sq = lax.psum(grad_sq, ("row", "col"))
    partner_sums = partner(jnp.stack([grad_sq, cond_sq]), "col", 0)
    block_grad = grad_sq + partner_sums[0]
    block_cond = cond_sq + partner_sums[1]
    block_count = BLK * BLK
    total_count = lax.axis_size("row") * lax.axis_size("col") // 2 * block_count
    clip_factor = clip_rms / jnp.sqrt(global_sq / total_count + epsilon)
    graft_ratio = jnp.sqrt(
        (block_grad / block_count + epsilon) / (block_cond / block_count + epsilon)
    )
    return (clip_factor * graft_ratio * preconditioned).astype(jnp.bfloat16)


def solution(mesh):
    placed = (P(("row", "col"), None), P(("row", "col"), None), P(("row", "col"), None))
    return jax.shard_map(
        shards, mesh=mesh, in_specs=placed, out_specs=P(("row", "col"), None), check_vma=False
    )
```

profile of v0, /device:TPU:0, one launch (start us, length us, event | category | flops | bytes accessed | tf_op | source)
XLA Modules:
  0.0 59.8 jit_solution(16291145906748680650)
XLA Ops:
  0.0 0.0 copy-start
  0.0 0.0 copy-start.1
  0.0 0.5 collective-permute-start
  0.5 2.1 %fusion.2 = f32[512,1024]{1,0:T(8,128)S(1)} fusion(bf16[512,1024]{1,0:T(8,128)(2,1)} %param.5, bf16[512,1024]{1,0:T(8,128)(2,1)} %param.3, s32[]{:T(128)S(6)} %select_n.16), kind=kOutput, calls=%fused_computation.7 | convolution fusion | flops 536870912 | bytes 3670020 | tf_op jit(solution)/shard_map/dot_general | solution.py:20
  2.6 0.5 collective-permute-done
  3.1 0.0 copy-done.1
  3.1 2.0 %add_convert_fusion = bf16[512,1024]{1,0:T(8,128)(2,1)S(1)} fusion(f32[512,1024]{1,0:T(8,128)S(1)} %fusion.2, bf16[512,1024]{1,0:T(8,128)(2,1)} %collective-permute-done, bf16[512,1024]{1,0:T(8,128)(2,1)S(1)} %copy-done.1, s32[]{:T(128)S(6)} %select_n.17), kind=kOutput, calls=%fused_computation.2 | convolution fusion | flops 537919488 | bytes 4718596 | tf_op jit(solution)/shard_map/dot_general | solution.py:21
  5.1 0.4 collective-permute-start.1
  5.5 1.2 %multiply_reduce_fusion.1 = f32[]{:T(128)} fusion(bf16[512,1024]{1,0:T(8,128)(2,1)S(1)} %copy-done.1), kind=kLoop, calls=%fused_computation.3 | loop fusion | flops 1572863 | bytes 1048580 | tf_op jit(solution)/shard_map/reduce_sum | solution.py:39
  6.7 41.8 %psum.7 = f32[]{:T(128)} all-reduce(f32[]{:T(128)} %multiply_reduce_fusion.1), channel_id=1, replica_groups=mesh['row'=8,'col'=4] {'row','col'}, use_global_device_ids=true, to_apply=%region_1.2 | all-reduce | flops 1 | bytes 8 | tf_op jit(solution)/shard_map/psum | solution.py:41
  49.3 0.0 copy-done
  49.3 0.7 %fusion.4 = f32[512,1024]{1,0:T(8,128)S(1)} fusion(bf16[512,1024]{1,0:T(8,128)(2,1)S(1)} %add_convert_fusion, bf16[512,1024]{1,0:T(8,128)(2,1)S(1)} %copy-done, s32[]{:T(128)S(6)} %select_n.16), kind=kOutput, calls=%fused_computation.9 | convolution fusion | flops 536870912 | bytes 3670020 | tf_op jit(solution)/shard_map/dot_general | solution.py:35
  50.0 0.0 collective-permute-done.1
  50.0 2.7 %multiply_reduce_fusion = (f32[]{:T(128)}, f32[512,1024]{1,0:T(8,128)S(1)}) fusion(f32[512,1024]{1,0:T(8,128)S(1)} %fusion.4, bf16[512,1024]{1,0:T(8,128)(2,1)} %collective-permute-done.1, bf16[512,1024]{1,0:T(8,128)(2,1)S(1)} %copy-done, s32[]{:T(128)S(6)} %select_n.17), kind=kOutput, calls=%fused_computation.1 | convolution fusion | flops 538443776 | bytes 5767176 | tf_op jit(solution)/shard_map/dot_general | solution.py:36
  52.7 1.4 %pad_maximum_fusion = f32[2]{0:T(128)S(1)} fusion(f32[1]{0:T(128)} %bitcast.1, f32[1]{0:T(128)} %bitcast), kind=kLoop, calls=%fused_computation.15 | loop fusion | flops 2 | bytes 16 | tf_op jit(solution)/shard_map/stack | solution.py:42
  54.1 0.0 collective-permute-start.2
  54.1 1.1 %collective-permute-done.2 = f32[2]{0:T(128)S(1)} collective-permute-done((f32[2]{0:T(128)S(1)}, f32[2]{0:T(128)S(1)}, u32[]{:S(2)}, u32[]{:S(2)}) %collective-permute-start.2) | collective-permute-done | bytes 40 | tf_op jit(solution)/shard_map/ppermute | solution.py:14
  55.3 0.7 %fusion.10 = (f32[1]{0:T(128)}, f32[1]{0:T(128)}) fusion(f32[2]{0:T(128)S(1)} %collective-permute-done.2), kind=kLoop, calls=%fused_computation.16 | loop fusion | bytes 16 | tf_op jit(solution)/shard_map/slice | solution.py:44
  58.6 1.2 %multiply_convert_fusion = bf16[512,1024]{1,0:T(8,128)(2,1)} fusion(f32[512,1024]{1,0:T(8,128)S(1)} %get-tuple-element.8, f32[]{:T(128)S(6)} %mul.21), kind=kLoop, calls=%fused_computation | loop fusion | flops 1048576 | bytes 3145732 | tf_op jit(solution)/shard_map/convert_element_type | solution.py:51
Async XLA Ops:
  0.0 49.3 %copy-start = (bf16[512,1024]{1,0:T(8,128)(2,1)S(1)}, bf16[512,1024]{1,0:T(8,128)(2,1)}, u32[]{:S(2)}) copy-start(bf16[512,1024]{1,0:T(8,128)(2,1)} %param.4) | copy-start | bytes 3145732
  0.0 3.1 %copy-start.1 = (bf16[512,1024]{1,0:T(8,128)(2,1)S(1)}, bf16[512,1024]{1,0:T(8,128)(2,1)}, u32[]{:S(2)}) copy-start(bf16[512,1024]{1,0:T(8,128)(2,1)} %param.3) | copy-start | bytes 3145732
  0.0 3.1 %collective-permute-start = (bf16[512,1024]{1,0:T(8,128)(2,1)}, bf16[512,1024]{1,0:T(8,128)(2,1)}, u32[]{:S(2)}, u32[]{:S(2)}) collective-permute-start(bf16[512,1024]{1,0:T(8,128)(2,1)} %param.5), channel_id=1, source_target_pairs={{0,1},{1,0},{2,3},{3,2},{4,5},{5,4},{6,7},{7,6},{8,9},{9,8},{10,11... | collective-permute-start | bytes 3145736 | tf_op jit(solution)/shard_map/ppermute | solution.py:14
  5.1 44.9 %collective-permute-start.1 = (bf16[512,1024]{1,0:T(8,128)(2,1)S(1)}, bf16[512,1024]{1,0:T(8,128)(2,1)}, u32[]{:S(2)}, u32[]{:S(2)}) collective-permute-start(bf16[512,1024]{1,0:T(8,128)(2,1)S(1)} %add_convert_fusion), channel_id=1, source_target_pairs={{0,1},{1,0},{2,3},{3,2},{4,5},{5,4},{6,7},{7,6},{8,9},{9,8},{10,11... | collective-permute-start | bytes 3145736 | tf_op jit(solution)/shard_map/ppermute | solution.py:14
  54.1 1.2 %collective-permute-start.2 = (f32[2]{0:T(128)S(1)}, f32[2]{0:T(128)S(1)}, u32[]{:S(2)}, u32[]{:S(2)}) collective-permute-start(f32[2]{0:T(128)S(1)} %pad_maximum_fusion), channel_id=1, source_target_pairs={{0,1},{1,0},{2,3},{3,2},{4,5},{5,4},{6,7},{7,6},{8,9},{9,8},{10,11... | collective-permute-start | bytes 32 | tf_op jit(solution)/shard_map/ppermute | solution.py:14
where the time goes:
time: 60.2 us; the launch traced here: 59.8 us
  blocking collectives  41.8 us (69%)
  matrix products  7.48 us (12%)
  other arithmetic  3.84 us (6%)
  between operations  3.42 us (6%)
  waiting for transfers between devices  1.68 us (3%)
  starting transfers between devices  0.94 us (2%)
  local copies, waits for them, and re-layouts  0.67 us (1%)
    psum x1, blocking collectives, shards(): global_sq = lax.psum(grad_sq, ('row', 'col'))  41.8 us
    dot_general x1, matrix products, shards(): jnp.dot(other_left, partner_rows, preferred_element_type=jnp.float32)  2.71 us
    dot_general x1, matrix products, apply_right(): applied = jnp.dot(own_cols, right_root, preferred_element_type=jnp.float32)  2.1 us
    dot_general x1, matrix products, apply_right(): jnp.dot(other_cols, partner_right, preferred_element_type=jnp.float32)  1.96 us
    ppermute x3, waiting for transfers between devices, partner(): lax.ppermute(shard, axis, [(i, i ^ 1 << distance) for i in range(lax.axis...  1.68 us
    another operation x1, other arithmetic, shards(): partner_sums = partner(jnp.stack([grad_sq, cond_sq]), 'col', 0)  1.41 us
    convert_element_type x1, other arithmetic, shards(): return (clip_factor * graft_ratio * preconditioned).astype(jnp.bfloat16)  1.22 us
    reduce_sum x1, other arithmetic, shards(): grad_sq = jnp.sum(jnp.square(grad.astype(jnp.float32)))  1.21 us
  transfers between devices with their start and end apart: 3, of which 2 were waited for; matrix products, arithmetic and copies ran while one was open for 7% of the time, Pallas kernels for 0%

commit v1 on v0

v1 whole, which is shorter than its diff:
```python
import functools

import jax
import jax.numpy as jnp
from jax import lax
from jax.experimental import pallas as pl
from jax.experimental.pallas import tpu as pltpu
from jax.sharding import PartitionSpec as P

epsilon = 1e-06
clip_rms = 1.0
MESH = pl.DeviceIdType.MESH
F32 = jnp.float32


def nn(a, b):
    return jnp.dot(a, b, preferred_element_type=F32)


def nt(a, b):
    return lax.dot_general(a, b, (((1,), (1,)), ((), ())), preferred_element_type=F32)


def row_sq(x):
    s = jnp.sum(x * x, axis=0, keepdims=True)
    total = s[:, :128]
    for i in range(128, s.shape[1], 128):
        total = total + s[:, i : i + 128]
    return total


def near_far(nr, nc):
    low = 2 if nr % 2 == 0 else 1
    near = [(x, c, b) for x in range(low) for c in range(nc // 2) for b in range(2)]
    far = list(range(nr // low))
    return low, near[1:], far[1:]


def kernel(nr, nc, g_hbm, l_hbm, r_hbm, p_ref, factor_ref,
           ga, gb, ra_own, ra_off, la, lb, rx, ra0, ra1, xa, xb, part,
           near_buf, far_buf, cond_buf, load_sem, send_sem, recv_sem):
    rows = g_hbm.shape[0]
    width = g_hbm.shape[1]
    row, col = lax.axis_index("row"), lax.axis_index("col")
    parity = lax.rem(col, 2)
    low, near, far = near_far(nr, nc)
    x_me, z_me, c_me = lax.rem(row, low), row // low, col // 2

    def near_id(k):
        x, c, b = k
        prow = z_me * low + lax.rem(x_me + x, low)
        pcol = lax.rem(c_me + c, nc // 2) * 2 + lax.rem(parity + b, 2)
        return (prow, pcol)

    def far_id(k):
        return (lax.rem(z_me + k, nr // low) * low + x_me, col)

    partner = (row, c_me * 2 + 1 - parity)

    barrier = pltpu.get_barrier_semaphore()
    for k in near:
        pl.semaphore_signal(barrier, inc=1, device_id=near_id(k), device_id_type=MESH)
    for k in far:
        pl.semaphore_signal(barrier, inc=1, device_id=far_id(k), device_id_type=MESH)

    own = pl.ds(pl.multiple_of(parity * rows, rows), rows)
    off = pl.ds(pl.multiple_of((1 - parity) * rows, rows), rows)
    loads = []
    for i, (src, where, dst) in enumerate(
        ((g_hbm, own, ga), (g_hbm, off, gb), (r_hbm, own, ra_own), (r_hbm, off, ra_off),
         (l_hbm, own, la), (l_hbm, off, lb))
    ):
        loads.append(pltpu.make_async_copy(src.at[:, where], dst, load_sem.at[i]))
        loads[-1].start()

    sends = []

    def send(src, dst, device):
        i = len(sends)
        copy = pltpu.make_async_remote_copy(
            src_ref=src, dst_ref=dst, send_sem=send_sem.at[i], recv_sem=recv_sem.at[i],
            device_id=device, device_id_type=MESH)
        copy.start()
        sends.append(copy)
        return copy

    loads[0].wait()
    sq = row_sq(ga[...].astype(F32))
    loads[1].wait()
    sq = sq + row_sq(gb[...].astype(F32))
    near_buf[0] = sq
    loads[2].wait()
    loads[3].wait()
    ra0[...] = (nn(ga[...], ra_own[...]) + nt(gb[...], ra_off[...])).astype(jnp.bfloat16)

    pl.semaphore_wait(barrier, len(near) + len(far))
    near_copies = [send(near_buf.at[0], near_buf.at[1 + i], near_id(k)) for i, k in enumerate(near)]
    rx_copy = send(ra_own, rx, partner)
    xb_copy = send(ra0, xb, partner)

    part[...] = nn(ga[...], ra_off[...])
    loads[4].wait()
    p_ref[:, own] = nn(la[...], ra0[...])
    rx_copy.wait_recv()
    ra1[...] = (part[...] + nn(gb[...], rx[...])).astype(jnp.bfloat16)
    xa_copy = send(ra1, xa, partner)
    part[...] = nn(la[...], ra1[...])

    block_row = sq
    near_sum = sq
    for i, (k, copy) in enumerate(zip(near, near_copies)):
        copy.wait_recv()
        near_sum = near_sum + near_buf[1 + i]
        if k == (0, 0, 1):
            block_row = sq + near_buf[1 + i]
    far_buf[0] = near_sum
    far_copies = [send(far_buf.at[0], far_buf.at[1 + i], far_id(k)) for i, k in enumerate(far)]

    loads[5].wait()
    xb_copy.wait_recv()
    p1 = part[...] + nn(lb[...], xb[...])
    p_ref[:, off] = p1
    cond = row_sq(p1)
    xa_copy.wait_recv()
    p0 = p_ref[:, own] + nn(lb[...], xa[...])
    p_ref[:, own] = p0
    cond = cond + row_sq(p0)
    cond_buf[0] = cond
    cond_copy = send(cond_buf.at[0], cond_buf.at[1], partner)

    total = near_sum
    for i, copy in enumerate(far_copies):
        copy.wait_recv()
        total = total + far_buf[1 + i]
    cond_copy.wait_recv()
    cond = cond + cond_buf[1]

    count = width * width
    global_sq = jnp.sum(total, axis=1, keepdims=True)
    grad_sq = jnp.sum(block_row, axis=1, keepdims=True)
    cond_sq = jnp.sum(cond, axis=1, keepdims=True)
    clip = clip_rms / jnp.sqrt(global_sq / (nr * nc * rows * width) + epsilon)
    graft = jnp.sqrt((grad_sq / count + epsilon) / (cond_sq / count + epsilon))
    factor_ref[...] = jnp.broadcast_to(clip * graft, factor_ref.shape)
    for copy in sends:
        copy.wait_send()


def shards(nr, nc, grad, left_root, right_root):
    rows, width = grad.shape
    low, near, far = near_far(nr, nc)
    copies = len(near) + len(far) + 4
    quarter = pltpu.VMEM((rows, width // 2), jnp.bfloat16)
    vmem = pl.BlockSpec(memory_space=pltpu.VMEM)
    preconditioned, factor = pl.pallas_call(
        functools.partial(kernel, nr, nc),
        out_shape=(jax.ShapeDtypeStruct((rows, width), F32), jax.ShapeDtypeStruct((8, 128), F32)),
        in_specs=[pl.BlockSpec(memory_space=pltpu.HBM)] * 3,
        out_specs=(vmem, vmem),
        scratch_shapes=[quarter] * 11
        + [
            pltpu.VMEM((rows, width // 2), F32),
            pltpu.VMEM((1 + len(near), 1, 128), F32),
            pltpu.VMEM((1 + len(far), 1, 128), F32),
            pltpu.VMEM((2, 1, 128), F32),
            pltpu.SemaphoreType.DMA((6,)),
            pltpu.SemaphoreType.DMA((copies,)),
            pltpu.SemaphoreType.DMA((copies,)),
        ],
        compiler_params=pltpu.CompilerParams(
            collective_id=0, has_side_effects=True, vmem_limit_bytes=64_900_000
        ),
        name="shampoo",
    )(grad, left_root, right_root)
    return (factor[0, 0] * preconditioned).astype(jnp.bfloat16)


def solution(mesh):
    placed = (P(("row", "col"), None), P(("row", "col"), None), P(("row", "col"), None))
    return jax.shard_map(
        functools.partial(shards, mesh.shape["row"], mesh.shape["col"]),
        mesh=mesh, in_specs=placed, out_specs=P(("row", "col"), None), check_vma=False
    )
```

time: 60.2 us -> 19.5 us (0.32)
  blocking collectives: 41.8 us -> 0 us
  Pallas kernels: 0 us -> 14.7 us
  matrix products: 7.48 us -> 0 us
  between operations: 3.42 us -> 0.01 us
  waiting for transfers between devices: 1.68 us -> 0 us
  starting transfers between devices: 0.94 us -> 0 us
    psum x1 -> x0, blocking collectives: 41.8 us -> none  [shards(): global_sq = lax.psum(grad_sq, ('row', 'col'))]
    pallas_call x0 -> x1, Pallas kernels: none -> 14.7 us  [shards(): pl.pallas_call(functools.partial(kernel, nr, nc), out_shape=(jax.ShapeDty...]
    dot_general x4 -> x0, matrix products: 7.48 us -> none  [the longest x1 2.71 us: shards(): jnp.dot(other_left, partner_rows, preferred_element_type=jnp.float32)]
    convert_element_type x1, other arithmetic: 1.22 us -> 3.42 us  [shards(): return (factor[0, 0] * preconditioned).astype(jnp.bfloat16)]
    ppermute x3 -> x0, waiting for transfers between devices: 1.68 us -> none  [partner(): lax.ppermute(shard, axis, [(i, i ^ 1 << distance) for i in range(lax.axis...]
    another operation x1 -> x0, other arithmetic: 1.41 us -> none  [shards(): partner_sums = partner(jnp.stack([grad_sq, cond_sq]), 'col', 0)]
    reduce_sum x1 -> x0, other arithmetic: 1.21 us -> none  [shards(): grad_sq = jnp.sum(jnp.square(grad.astype(jnp.float32)))]
    ppermute x3 -> x0, starting transfers between devices: 0.94 us -> none  [partner(): lax.ppermute(shard, axis, [(i, i ^ 1 << distance) for i in range(lax.axis...]
  transfers between devices with their start and end apart: 3 -> 0, of which waited for: 2 -> 0; matrix products, arithmetic and copies ran while one was open for 7% -> 0% of each run, Pallas kernels for 0% -> 0%
where the time goes in v1:
time: 19.5 us; the launch traced here: 19.3 us
  Pallas kernels  14.7 us (75%)
  other arithmetic  3.42 us (18%)
  local copies, waits for them, and re-layouts  1.19 us (6%)
    pallas_call x1, Pallas kernels, shards(): pl.pallas_call(functools.partial(kernel, nr, nc), out_shape=(jax.ShapeDty...  14.7 us
    convert_element_type x1, other arithmetic, shards(): return (factor[0, 0] * preconditioned).astype(jnp.bfloat16)  3.42 us
    slice x1, local copies, waits for them, and re-layouts, shards(): return (factor[0, 0] * preconditioned).astype(jnp.bfloat16)  1.19 us

profile of v1, /device:TPU:0, one launch (start us, length us, event | category | flops | bytes accessed | tf_op | source)
XLA Modules:
  0.0 19.3 jit_solution(6979709089578616297)
XLA Ops:
  0.0 14.7 %shampoo.1 = (f32[512,1024]{1,0:T(8,128)}, f32[8,128]{1,0:T(8,128)}) custom-call(bf16[512,1024]{1,0:T(8,128)(2,1)} %g_hbm.1, bf16[512,1024]{1,0:T(8,128)(2,1)} %l_hbm.1, bf16[512,1024]{1,0:T(8,128)(2,1)} %r_hbm.1), custom_call_target="tpu_custom_call" | custom-call | tf_op jit(solution)/shard_map/shampoo/pallas_call | solution.py:155
  14.7 1.2 %slice.3 = f32[1,1]{1,0:T(1,128)} slice(f32[8,128]{1,0:T(8,128)} %get-tuple-element.7), slice={[0:1], [0:1]} | slice | bytes 8 | tf_op jit(solution)/shard_map/slice | solution.py:175
  15.9 3.4 %multiply_convert_fusion = bf16[512,1024]{1,0:T(8,128)(2,1)} fusion(f32[512,1024]{1,0:T(8,128)} %get-tuple-element.8, f32[]{:T(128)} %bitcast), kind=kLoop, calls=%fused_computation | loop fusion | flops 1048576 | bytes 3145732 | tf_op jit(solution)/shard_map/convert_element_type | solution.py:175

commit v2 on v1

--- a/solution.py
+++ b/solution.py
@@ -146,15 +146,34 @@
         copy.wait_send()
 
 
+CHUNKS = 4
+
+
+def scale(p_ref, factor_ref, out_hbm, scaled, sem):
+    rows = p_ref.shape[0] // CHUNKS
+    factor = factor_ref[0:1, 0:1]
+    copies = []
+    for i in range(CHUNKS):
+        part = pl.ds(i * rows, rows)
+        scaled[part, :] = (factor * p_ref[part, :]).astype(jnp.bfloat16)
+        copies.append(pltpu.make_async_copy(scaled.at[part, :], out_hbm.at[part, :], sem.at[i]))
+        copies[-1].start()
+    for copy in copies:
+        copy.wait()
+
+
 def shards(nr, nc, grad, left_root, right_root):
     rows, width = grad.shape
     low, near, far = near_far(nr, nc)
     copies = len(near) + len(far) + 4
     quarter = pltpu.VMEM((rows, width // 2), jnp.bfloat16)
     vmem = pl.BlockSpec(memory_space=pltpu.VMEM)
+    grad, left_root, right_root = (
+        pltpu.with_memory_space_constraint(a, pltpu.HBM) for a in (grad, left_root, right_root)
+    )
     preconditioned, factor = pl.pallas_call(
         functools.partial(kernel, nr, nc),
-        out_shape=(jax.ShapeDtypeStruct((rows, width), F32), jax.ShapeDtypeStruct((8, 128), F32)),
+        out_shape=(pltpu.VMEM((rows, width), F32), pltpu.VMEM((1, 128), F32)),
         in_specs=[pl.BlockSpec(memory_space=pltpu.HBM)] * 3,
         out_specs=(vmem, vmem),
         scratch_shapes=[quarter] * 11
@@ -168,11 +187,19 @@
             pltpu.SemaphoreType.DMA((copies,)),
         ],
         compiler_params=pltpu.CompilerParams(
-            collective_id=0, has_side_effects=True, vmem_limit_bytes=64_900_000
+            collective_id=0, has_side_effects=True, vmem_limit_bytes=32 * 1024 * 1024
         ),
         name="shampoo",
     )(grad, left_root, right_root)
-    return (factor[0, 0] * preconditioned).astype(jnp.bfloat16)
+    return pl.pallas_call(
+        scale,
+        out_shape=jax.ShapeDtypeStruct((rows, width), jnp.bfloat16),
+        in_specs=[vmem, vmem],
+        out_specs=pl.BlockSpec(memory_space=pltpu.HBM),
+        scratch_shapes=[pltpu.VMEM((rows, width), jnp.bfloat16), pltpu.SemaphoreType.DMA((CHUNKS,))],
+        compiler_params=pltpu.CompilerParams(vmem_limit_bytes=16 * 1024 * 1024),
+        name="scale",
+    )(preconditioned, factor)
 
 
 def solution(mesh):

time: 19.5 us -> 14.6 us (0.75)
  other arithmetic: 3.42 us -> 0 us
  local copies, waits for them, and re-layouts: 1.19 us -> 0 us
  Pallas kernels: 14.7 us -> 14.4 us
    convert_element_type x1 -> x0, other arithmetic: 3.42 us -> none  [shards(): return (factor[0, 0] * preconditioned).astype(jnp.bfloat16)]
    slice x1 -> x0, local copies, waits for them, and re-layouts: 1.19 us -> none  [shards(): return (factor[0, 0] * preconditioned).astype(jnp.bfloat16)]
    pallas_call x1 -> x2, Pallas kernels: 14.7 us -> 14.4 us  [the longest x1 13.3 us: shards(): pl.pallas_call(functools.partial(kernel, nr, nc), out_shape=(pltpu.VMEM((...]
where the time goes in v2:
time: 14.6 us; the launch traced here: 14.5 us
  Pallas kernels  14.4 us (99%)
    pallas_call x1, Pallas kernels, shards(): pl.pallas_call(functools.partial(kernel, nr, nc), out_shape=(pltpu.VMEM((...  13.3 us
    pallas_call x1, Pallas kernels, shards(): pl.pallas_call(scale, out_shape=jax.ShapeDtypeStruct((rows, width), jnp.b...  1.11 us

profile of v2, /device:TPU:0, one launch (start us, length us, event | category | flops | bytes accessed | tf_op | source)
XLA Modules:
  0.0 14.5 jit_solution(9351498406450065961)
XLA Ops:
  0.0 13.3 %shampoo.1 = (f32[512,1024]{1,0:T(8,128)S(1)}, f32[1,128]{1,0:T(1,128)S(1)}) custom-call(bf16[512,1024]{1,0:T(8,128)(2,1)} %g_hbm.1, bf16[512,1024]{1,0:T(8,128)(2,1)} %l_hbm.1, bf16[512,1024]{1,0:T(8,128)(2,1)} %r_hbm.1), custom_call_target="tpu_custom_call" | custom-call | tf_op jit(solution)/shard_map/shampoo/pallas_call | solution.py:174
  13.3 1.1 %scale.1 = bf16[512,1024]{1,0:T(8,128)(2,1)} custom-call(f32[512,1024]{1,0:T(8,128)S(1)} %get-tuple-element.7.p_ref, f32[1,128]{1,0:T(1,128)S(1)} %get-tuple-element.8.factor_ref), custom_call_target="tpu_custom_call" | custom-call | tf_op jit(solution)/shard_map/scale/pallas_call | solution.py:194

commit v3 on v2

--- a/solution.py
+++ b/solution.py
@@ -29,39 +29,18 @@
     return total
 
 
-def near_far(nr, nc):
-    low = 2 if nr % 2 == 0 else 1
-    near = [(x, c, b) for x in range(low) for c in range(nc // 2) for b in range(2)]
-    far = list(range(nr // low))
-    return low, near[1:], far[1:]
-
-
 def kernel(nr, nc, g_hbm, l_hbm, r_hbm, p_ref, factor_ref,
            ga, gb, ra_own, ra_off, la, lb, rx, ra0, ra1, xa, xb, part,
-           near_buf, far_buf, cond_buf, load_sem, send_sem, recv_sem):
-    rows = g_hbm.shape[0]
-    width = g_hbm.shape[1]
+           sums, pair, load_sem, send_sem, recv_sem, sums_send, sums_recv, ready):
+    rows, width = g_hbm.shape
+    devices = nr * nc
     row, col = lax.axis_index("row"), lax.axis_index("col")
     parity = lax.rem(col, 2)
-    low, near, far = near_far(nr, nc)
-    x_me, z_me, c_me = lax.rem(row, low), row // low, col // 2
-
-    def near_id(k):
-        x, c, b = k
-        prow = z_me * low + lax.rem(x_me + x, low)
-        pcol = lax.rem(c_me + c, nc // 2) * 2 + lax.rem(parity + b, 2)
-        return (prow, pcol)
-
-    def far_id(k):
-        return (lax.rem(z_me + k, nr // low) * low + x_me, col)
-
-    partner = (row, c_me * 2 + 1 - parity)
-
-    barrier = pltpu.get_barrier_semaphore()
-    for k in near:
-        pl.semaphore_signal(barrier, inc=1, device_id=near_id(k), device_id_type=MESH)
-    for k in far:
-        pl.semaphore_signal(barrier, inc=1, device_id=far_id(k), device_id_type=MESH)
+    me = row * nc + col
+    partner = (row, col + 1 - 2 * parity)
+
+    def place(rank):
+        return (lax.div(rank, nc), lax.rem(rank, nc))
 
     own = pl.ds(pl.multiple_of(parity * rows, rows), rows)
     off = pl.ds(pl.multiple_of((1 - parity) * rows, rows), rows)
@@ -73,6 +52,20 @@
         loads.append(pltpu.make_async_copy(src.at[:, where], dst, load_sem.at[i]))
         loads[-1].start()
 
+    barrier = pltpu.get_barrier_semaphore()
+
+    def greet(rank, _):
+        pl.semaphore_signal(barrier, inc=1, device_id=place(rank), device_id_type=MESH)
+
+    lax.fori_loop(me - parity, me, greet, None)
+    lax.fori_loop(me + 1, devices, greet, None)
+    pl.semaphore_wait(barrier, me + 1 - parity)
+
+    def say_ready(rank, _):
+        pl.semaphore_signal(ready, inc=1, device_id=place(rank), device_id_type=MESH)
+
+    lax.fori_loop(0, me, say_ready, None)
+
     sends = []
 
     def send(src, dst, device):
@@ -84,18 +77,21 @@
         sends.append(copy)
         return copy
 
+    def send_sum(rank, _):
+        pltpu.make_async_remote_copy(
+            src_ref=pair.at[0], dst_ref=sums.at[me], send_sem=sums_send, recv_sem=sums_recv,
+            device_id=place(rank), device_id_type=MESH).start()
+
     loads[0].wait()
     sq = row_sq(ga[...].astype(F32))
     loads[1].wait()
     sq = sq + row_sq(gb[...].astype(F32))
-    near_buf[0] = sq
+    pair[0] = sq
+    lax.fori_loop(0, me, send_sum, None)
     loads[2].wait()
+    rx_copy = send(ra_own, rx, partner)
     loads[3].wait()
     ra0[...] = (nn(ga[...], ra_own[...]) + nt(gb[...], ra_off[...])).astype(jnp.bfloat16)
-
-    pl.semaphore_wait(barrier, len(near) + len(far))
-    near_copies = [send(near_buf.at[0], near_buf.at[1 + i], near_id(k)) for i, k in enumerate(near)]
-    rx_copy = send(ra_own, rx, partner)
     xb_copy = send(ra0, xb, partner)
 
     part[...] = nn(ga[...], ra_off[...])
@@ -105,16 +101,6 @@
     ra1[...] = (part[...] + nn(gb[...], rx[...])).astype(jnp.bfloat16)
     xa_copy = send(ra1, xa, partner)
     part[...] = nn(la[...], ra1[...])
-
-    block_row = sq
-    near_sum = sq
-    for i, (k, copy) in enumerate(zip(near, near_copies)):
-        copy.wait_recv()
-        near_sum = near_sum + near_buf[1 + i]
-        if k == (0, 0, 1):
-            block_row = sq + near_buf[1 + i]
-    far_buf[0] = near_sum
-    far_copies = [send(far_buf.at[0], far_buf.at[1 + i], far_id(k)) for i, k in enumerate(far)]
 
     loads[5].wait()
     xb_copy.wait_recv()
@@ -125,25 +111,30 @@
     p0 = p_ref[:, own] + nn(lb[...], xa[...])
     p_ref[:, own] = p0
     cond = cond + row_sq(p0)
-    cond_buf[0] = cond
-    cond_copy = send(cond_buf.at[0], cond_buf.at[1], partner)
-
-    total = near_sum
-    for i, copy in enumerate(far_copies):
-        copy.wait_recv()
-        total = total + far_buf[1 + i]
-    cond_copy.wait_recv()
-    cond = cond + cond_buf[1]
+    pair[1] = cond
+    pair_copy = send(pair.at[pl.ds(0, 2)], pair.at[pl.ds(2, 2)], partner)
+
+    @pl.when(me < devices - 1)
+    def _():
+        pl.semaphore_wait(ready, devices - 1 - me)
+        lax.fori_loop(me + 1, devices, send_sum, None)
+
 
     count = width * width
-    global_sq = jnp.sum(total, axis=1, keepdims=True)
-    grad_sq = jnp.sum(block_row, axis=1, keepdims=True)
-    cond_sq = jnp.sum(cond, axis=1, keepdims=True)
-    clip = clip_rms / jnp.sqrt(global_sq / (nr * nc * rows * width) + epsilon)
+    pair_copy.wait_recv()
+    grad_sq = jnp.sum(sq + pair[2], axis=1, keepdims=True)
+    cond_sq = jnp.sum(cond + pair[3], axis=1, keepdims=True)
     graft = jnp.sqrt((grad_sq / count + epsilon) / (cond_sq / count + epsilon))
-    factor_ref[...] = jnp.broadcast_to(clip * graft, factor_ref.shape)
     for copy in sends:
         copy.wait_send()
+
+    sums[me] = sq
+    others = pl.ds(0, devices - 1)
+    pltpu.make_async_copy(sums.at[others], sums.at[others], sums_recv).wait()
+    global_sq = jnp.sum(jnp.sum(sums[...], axis=0), axis=1, keepdims=True)
+    clip = clip_rms / jnp.sqrt(global_sq / (devices * rows * width) + epsilon)
+    factor_ref[...] = jnp.broadcast_to(clip * graft, factor_ref.shape)
+    pltpu.make_async_copy(sums.at[others], sums.at[others], sums_send).wait()
 
 
 CHUNKS = 4
@@ -164,8 +155,6 @@
 
 def shards(nr, nc, grad, left_root, right_root):
     rows, width = grad.shape
-    low, near, far = near_far(nr, nc)
-    copies = len(near) + len(far) + 4
     quarter = pltpu.VMEM((rows, width // 2), jnp.bfloat16)
     vmem = pl.BlockSpec(memory_space=pltpu.VMEM)
     grad, left_root, right_root = (
@@ -179,12 +168,14 @@
         scratch_shapes=[quarter] * 11
         + [
             pltpu.VMEM((rows, width // 2), F32),
-            pltpu.VMEM((1 + len(near), 1, 128), F32),
-            pltpu.VMEM((1 + len(far), 1, 128), F32),
-            pltpu.VMEM((2, 1, 128), F32),
+            pltpu.VMEM((nr * nc, 1, 128), F32),
+            pltpu.VMEM((4, 1, 128), F32),
             pltpu.SemaphoreType.DMA((6,)),
-            pltpu.SemaphoreType.DMA((copies,)),
-            pltpu.SemaphoreType.DMA((copies,)),
+            pltpu.SemaphoreType.DMA((4,)),
+            pltpu.SemaphoreType.DMA((4,)),
+            pltpu.SemaphoreType.DMA,
+            pltpu.SemaphoreType.DMA,
+            pltpu.SemaphoreType.REGULAR,
         ],
         compiler_params=pltpu.CompilerParams(
             collective_id=0, has_side_effects=True, vmem_limit_bytes=32 * 1024 * 1024

time: 14.6 us -> 11.3 us (0.77)
  Pallas kernels: 14.4 us -> 11.1 us
    pallas_call x1, Pallas kernels: 13.3 us -> 10 us  [shards(): pl.pallas_call(functools.partial(kernel, nr, nc), out_shape=(pltpu.VMEM((...]
where the time goes in v3:
time: 11.3 us; the launch traced here: 11.2 us
  Pallas kernels  11.1 us (98%)
    pallas_call x1, Pallas kernels, shards(): pl.pallas_call(functools.partial(kernel, nr, nc), out_shape=(pltpu.VMEM((...  10 us
    pallas_call x1, Pallas kernels, shards(): pl.pallas_call(scale, out_shape=jax.ShapeDtypeStruct((rows, width), jnp.b...  1.11 us

profile of v3, /device:TPU:0, one launch (start us, length us, event | category | flops | bytes accessed | tf_op | source)
XLA Modules:
  0.0 11.2 jit_solution(12415831242395156219)
XLA Ops:
  0.0 10.0 %shampoo.1 = (f32[512,1024]{1,0:T(8,128)S(1)}, f32[1,128]{1,0:T(1,128)S(1)}) custom-call(bf16[512,1024]{1,0:T(8,128)(2,1)} %g_hbm.1, bf16[512,1024]{1,0:T(8,128)(2,1)} %l_hbm.1, bf16[512,1024]{1,0:T(8,128)(2,1)} %r_hbm.1), custom_call_target="tpu_custom_call" | custom-call | tf_op jit(solution)/shard_map/shampoo/pallas_call | solution.py:163
  10.0 1.1 %scale.1 = bf16[512,1024]{1,0:T(8,128)(2,1)} custom-call(f32[512,1024]{1,0:T(8,128)S(1)} %get-tuple-element.7.p_ref, f32[1,128]{1,0:T(1,128)S(1)} %get-tuple-element.8.factor_ref), custom_call_target="tpu_custom_call" | custom-call | tf_op jit(solution)/shard_map/scale/pallas_call | solution.py:185

commit v4 on v3

--- a/solution.py
+++ b/solution.py
@@ -29,11 +29,16 @@
     return total
 
 
+def group_size(nr, nc):
+    return (2 if nr % 2 == 0 else 1) * nc
+
+
 def kernel(nr, nc, g_hbm, l_hbm, r_hbm, p_ref, factor_ref,
            ga, gb, ra_own, ra_off, la, lb, rx, ra0, ra1, xa, xb, part,
            sums, pair, load_sem, send_sem, recv_sem, sums_send, sums_recv, ready):
     rows, width = g_hbm.shape
     devices = nr * nc
+    members = group_size(nr, nc)
     row, col = lax.axis_index("row"), lax.axis_index("col")
     parity = lax.rem(col, 2)
     me = row * nc + col
@@ -50,7 +55,8 @@
          (l_hbm, own, la), (l_hbm, off, lb))
     ):
         loads.append(pltpu.make_async_copy(src.at[:, where], dst, load_sem.at[i]))
-        loads[-1].start()
+        if i < 4:
+            loads[-1].start()
 
     barrier = pltpu.get_barrier_semaphore()
 
@@ -62,7 +68,7 @@
     pl.semaphore_wait(barrier, me + 1 - parity)
 
     def say_ready(rank, _):
-        pl.semaphore_signal(ready, inc=1, device_id=place(rank), device_id_type=MESH)
+        pl.semaphore_signal(ready.at[lax.div(me, members)], inc=1, device_id=place(rank), device_id_type=MESH)
 
     lax.fori_loop(0, me, say_ready, None)
 
@@ -87,12 +93,16 @@
     loads[1].wait()
     sq = sq + row_sq(gb[...].astype(F32))
     pair[0] = sq
-    lax.fori_loop(0, me, send_sum, None)
+    loads[4].start()
+    loads[5].start()
+    head = jnp.minimum(me, 2)
+    lax.fori_loop(0, head, send_sum, None)
     loads[2].wait()
     rx_copy = send(ra_own, rx, partner)
     loads[3].wait()
     ra0[...] = (nn(ga[...], ra_own[...]) + nt(gb[...], ra_off[...])).astype(jnp.bfloat16)
     xb_copy = send(ra0, xb, partner)
+    lax.fori_loop(head, me, send_sum, None)
 
     part[...] = nn(ga[...], ra_off[...])
     loads[4].wait()
@@ -101,6 +111,17 @@
     ra1[...] = (part[...] + nn(gb[...], rx[...])).astype(jnp.bfloat16)
     xa_copy = send(ra1, xa, partner)
     part[...] = nn(la[...], ra1[...])
+
+    def send_up(group, _):
+        first = jnp.maximum(me + 1, group * members)
+        end = (group + 1) * members
+
+        @pl.when(first < end)
+        def _():
+            pl.semaphore_wait(ready.at[group], end - first)
+            lax.fori_loop(first, end, send_sum, None)
+
+    lax.fori_loop(lax.div(me, members), devices // members, send_up, None)
 
     loads[5].wait()
     xb_copy.wait_recv()
@@ -113,11 +134,6 @@
     cond = cond + row_sq(p0)
     pair[1] = cond
     pair_copy = send(pair.at[pl.ds(0, 2)], pair.at[pl.ds(2, 2)], partner)
-
-    @pl.when(me < devices - 1)
-    def _():
-        pl.semaphore_wait(ready, devices - 1 - me)
-        lax.fori_loop(me + 1, devices, send_sum, None)
 
 
     count = width * width
@@ -175,7 +191,7 @@
             pltpu.SemaphoreType.DMA((4,)),
             pltpu.SemaphoreType.DMA,
             pltpu.SemaphoreType.DMA,
-            pltpu.SemaphoreType.REGULAR,
+            pltpu.SemaphoreType.REGULAR((nr * nc // group_size(nr, nc),)),
         ],
         compiler_params=pltpu.CompilerParams(
             collective_id=0, has_side_effects=True, vmem_limit_bytes=32 * 1024 * 1024

time: 11.3 us -> 11.3 us (level)
  no operation moved by 1% of the time
where the time goes in v4:
time: 11.3 us; the launch traced here: 11.2 us
  Pallas kernels  11.2 us (99%)
    pallas_call x1, Pallas kernels, shards(): pl.pallas_call(functools.partial(kernel, nr, nc), out_shape=(pltpu.VMEM((...  10.1 us
    pallas_call x1, Pallas kernels, shards(): pl.pallas_call(scale, out_shape=jax.ShapeDtypeStruct((rows, width), jnp.b...  1.11 us

profile of v4, /device:TPU:0, one launch (start us, length us, event | category | flops | bytes accessed | tf_op | source)
XLA Modules:
  0.0 11.2 jit_solution(17680057221451125438)
XLA Ops:
  0.0 10.1 %shampoo.1 = (f32[512,1024]{1,0:T(8,128)S(1)}, f32[1,128]{1,0:T(1,128)S(1)}) custom-call(bf16[512,1024]{1,0:T(8,128)(2,1)} %g_hbm.1, bf16[512,1024]{1,0:T(8,128)(2,1)} %l_hbm.1, bf16[512,1024]{1,0:T(8,128)(2,1)} %r_hbm.1), custom_call_target="tpu_custom_call" | custom-call | tf_op jit(solution)/shard_map/shampoo/pallas_call | solution.py:179
  10.1 1.1 %scale.1 = bf16[512,1024]{1,0:T(8,128)(2,1)} custom-call(f32[512,1024]{1,0:T(8,128)S(1)} %get-tuple-element.7.p_ref, f32[1,128]{1,0:T(1,128)S(1)} %get-tuple-element.8.factor_ref), custom_call_target="tpu_custom_call" | custom-call | tf_op jit(solution)/shard_map/scale/pallas_call | solution.py:201
